TPU v7x, 128 devices: a whole 4x4x4 slice. The times are simulated.
128 devices in a mesh: expert: 8 (over z, core), fsdp: 16 (over y, x).
Axes of the slice: x: 4, y: 4, z: 4, core: 2. Of those that a mesh axis runs over, the one named last changes fastest.
Arguments:
- hidden: bfloat16 [8, 768, 8192], P('expert', None, 'fsdp'), may hold values from -0.198873782 to 0.198873782
- expert_ids: int32 [2048, 2], P(('expert', 'fsdp')), may hold values from 0 to 7, all different within a row; in each aligned block of 16 rows (0 to 15, 16 to 31, ...) at most 6 rows name the same one
- gate_weights: float32 [2048, 2], P(('expert', 'fsdp')), may hold values from 0.2 to 1
- loss_weight: float32 [2048], P(('expert', 'fsdp')), may hold values from 0.3 to 3
- decay: float32 [1], replicated, may hold values from 0.2 to 0.6
- val_grad: bfloat16 [8, 8192, 4096], P('expert', 'fsdp'), may hold values from -8 to 8
- down_weight: bfloat16 [8, 8192, 4096], P('expert', 'fsdp'), may hold values from -0.0625 to 0.0625
Outputs:
- solution: float32 [8, 8192, 4096], P('expert', 'fsdp')
- hyper: float32 [1], replicated
Inputs may be any that keep to these rules, and one draw needn't show every extreme that they name: `expert_ids`: each token names 2 different experts; among the 16 tokens of one device no expert is named more than 6 times, a bound that some block reaches.
All inputs are finite; a program needn't handle non-finite values.
Results may differ from a plain program's by a relative error of at most 0.00067.
Values may be sent and summed in bfloat16 or wider, within the bound.
No kernel may reach another device: no remote copies, remote signals or barrier semaphores. Data moves between devices by JAX's collectives and lax.ppermute only.
A program may use at most 128 MiB of HBM per device.

v0:
```python
import math
import jax
import jax.numpy as jnp
from jax import lax
from jax.sharding import Mesh
from jax.sharding import PartitionSpec as P

D = 4096
ITERS = 2
EXPERT_FSDP = ("expert_0", "expert_1", "fsdp_0", "fsdp_1")
EXPERT = ("expert_0", "expert_1")
FSDP = ("fsdp_0", "fsdp_1")


def by_axis(array, axes):
    for axis in axes:
        array = lax.psum(array, axis)
    return array


def gate_table(expert_ids, gate_weights, experts, capacity):
    flat_ids = expert_ids.reshape(-1)
    labels = jnp.arange(experts, dtype=jnp.int32)
    onehot = (flat_ids[:, None] == labels[None, :]).astype(jnp.int32)
    earlier = jnp.cumsum(onehot, axis=0) - onehot
    slots = jnp.sum(earlier * onehot, axis=1)
    targets = flat_ids * capacity + slots
    columns = jnp.arange(experts * capacity, dtype=jnp.int32)
    hits = (targets[:, None] == columns[None, :]).astype(jnp.float32)
    weighted = hits * gate_weights.reshape(-1)[:, None]
    return jnp.sum(weighted.reshape(-1, expert_ids.shape[1], experts * capacity), axis=1)


def combine(table, weights, outputs):
    mixed = jnp.dot(
        table, outputs, precision=lax.Precision.HIGHEST, preferred_element_type=jnp.float32
    )
    scaled = weights[:, None] * mixed
    back = jnp.dot(
        table.T, scaled, precision=lax.Precision.HIGHEST, preferred_element_type=jnp.float32
    )
    return back.astype(jnp.bfloat16)


def joined_sums(residual, direction, image, target):
    return (
        by_axis(jnp.sum(residual * residual), EXPERT_FSDP),
        by_axis(jnp.sum(direction * image), EXPERT_FSDP),
        by_axis(jnp.sum(residual * image), EXPERT_FSDP),
        by_axis(jnp.sum(image * image), EXPERT_FSDP),
        by_axis(jnp.sum(target.astype(jnp.float32) * direction), EXPERT_FSDP),
    )


def local(hidden, expert_ids, gate_weights, loss_weight, decay, val_grad, down_weight):
    n_expert = lax.axis_size(EXPERT)
    n_fsdp = lax.axis_size(FSDP)
    capacity = hidden.shape[1] // (n_expert * n_fsdp)
    decay_rate = decay[0]
    table = gate_table(expert_ids, gate_weights, n_expert, capacity)
    local_hidden = hidden[0]
    right_side, target = (val_grad, down_weight)
    start_side = right_side.astype(jnp.float32)
    solution = jnp.zeros_like(start_side)
    residual = start_side
    direction = start_side
    along_total = jnp.float32(0.0)
    for iteration in range(ITERS):
        if iteration > 0:
            direction = residual + norm_guess / norm_prev * direction
        rounded = direction[0].astype(jnp.bfloat16)
        summed = lax.psum_scatter(
            jnp.dot(local_hidden, rounded, preferred_element_type=jnp.float32),
            FSDP,
            scatter_dimension=0,
            tiled=True,
        )
        arrived = lax.all_to_all(summed, EXPERT, split_axis=0, concat_axis=0, tiled=True)
        leaving = combine(table, loss_weight, arrived)
        returned = lax.all_to_all(leaving, EXPERT, split_axis=0, concat_axis=0, tiled=True)
        gradient = lax.dot_general(
            local_hidden,
            lax.all_gather(returned, FSDP, axis=0, tiled=True),
            (((0,), (0,)), ((), ())),
            preferred_element_type=jnp.float32,
        )
        image = gradient[None] + decay_rate * direction
        norm_now, curve, cross, square, along = joined_sums(residual, direction, image, target)
        alpha = norm_now / curve
        solution = solution + alpha * direction
        residual = residual - alpha * image
        norm_guess = norm_now - 2.0 * alpha * cross + alpha * alpha * square
        norm_prev = norm_now
        along_total = along_total + alpha * along
    hyper = -along_total / math.sqrt(n_expert * D)
    return (solution, jnp.reshape(hyper, (1,)))


def solution(mesh):
    finer = Mesh(mesh.devices.reshape(4, 2, 4, 4), ("expert_0", "expert_1", "fsdp_0", "fsdp_1"))
    placed = (
        P(EXPERT, None, FSDP),
        P(EXPERT_FSDP, None),
        P(EXPERT_FSDP, None),
        P(EXPERT_FSDP),
        P(),
        P(EXPERT, FSDP, None),
        P(EXPERT, FSDP, None),
    )
    return jax.shard_map(
        local, mesh=finer, in_specs=placed, out_specs=(P(EXPERT, FSDP, None), P()), check_vma=False
    )
```

profile of v0, /device:TPU:0, one launch (start us, length us, event | category | flops | bytes accessed | tf_op | source)
XLA Modules:
  0.0 544.2 jit_solution(16271983358100491739)
XLA Ops:
  7.2 0.0 copy-start
  7.2 0.0 reduce-scatter.5.cloned.1.call-start
  7.2 1.1 copy-done
  8.3 8.6 %fusion.10 = f32[768,4096]{1,0:T(8,128)} fusion(bf16[1,512,4096]{2,1,0:T(8,128)(2,1)} %param.12, bf16[1,768,512]{2,1,0:T(8,128)(2,1)S(1)} %copy-done), kind=kOutput, calls=%fused_computation.26 | convolution fusion | flops 3221225472 | bytes 17563648 | tf_op jit(solution)/shard_map/dot_general | solution.py:73
  16.9 0.0 copy-start.1
  16.9 0.0 copy-start.3
  16.9 0.0 copy-start.2
  16.9 0.0 reduce-scatter.5.cloned.1.call-update
  16.9 97.7 %reduce-scatter.5.cloned.1.call-done = f32[48,4096]{1,0:T(8,128)} async-done(((f32[768,4096]{1,0:T(8,128)}), f32[48,4096]{1,0:T(8,128)}) %reduce-scatter.5.cloned.1.call-update) | async-done | bytes 786448 | tf_op jit(solution)/shard_map/reduce_scatter | solution.py:72
  114.5 2.2 all_to_all.32
  116.7 4.4 all-to-all-start
  121.2 0.0 all-gather.3.cloned.1.call-start
  121.2 0.0 copy-done.1
  121.2 0.1 copy.41
  121.3 0.1 eq.29
  121.4 0.1 fusion.17
  121.5 0.1 reduce_window_sum.11
  121.5 0.2 select_reduce_fusion.1
  121.7 0.1 reduce_sum.89
  121.8 0.1 copy.42
  121.9 0.0 copy-done.3
  121.9 0.1 select_reduce_fusion
  122.0 15.1 %all-to-all-done = f32[8,6,4096]{2,1,0:T(8,128)S(1)} async-done(((f32[8,6,4096]{2,1,0:T(8,128)}), f32[8,6,4096]{2,1,0:T(8,128)S(1)}, u32[]{:S(2)}, u32[]{:S(2)}) %all-to-all-start) | async-done | bytes 786464 | tf_op jit(solution)/shard_map/all_to_all | solution.py:78
  137.1 0.1 all_to_all.34
  137.2 0.0 copy-done.2
  137.2 0.5 convolution_multiply_fusion.1
  137.7 0.8 convolution_convert_fusion.1
  138.6 0.1 all_to_all.35
  138.7 12.8 %all_to_all.48 = bf16[8,6,4096]{2,1,0:T(8,128)(2,1)S(1)} all-to-all(bf16[8,6,4096]{2,1,0:T(8,128)(2,1)S(1)} %all_to_all.35), channel_id=1, replica_groups=mesh['expert_0'=4,'expert_1'=2,'fsdp_0'=4,'fsdp_1'=4] {'expert_0','exper..., dimensions={0} | all-to-all | bytes 786432 | tf_op jit(solution)/shard_map/all_to_all | solution.py:80
  151.5 0.9 all_to_all.37
  152.3 0.0 all-gather.3.cloned.1.call-update
  152.4 0.0 reduce-scatter.7.cloned.1.call-start
  152.4 6.5 %copy.40 = bf16[1,512,4096]{1,2,0:T(8,128)(2,1)} copy(bf16[1,512,4096]{2,1,0:T(8,128)(2,1)} %param.12) | data formatting | bytes 8388608 | tf_op args[5]
  159.6 51.1 %all-gather.3.cloned.1.call-done = bf16[768,4096]{1,0:T(8,128)(2,1)} async-done(((bf16[48,4096]{1,0:T(8,128)(2,1)}), bf16[768,4096]{1,0:T(8,128)(2,1)}) %all-gather.3.cloned.1.call-update) | async-done | bytes 6291472 | tf_op jit(solution)/shard_map/all_gather | solution.py:83
  210.7 12.3 %multiply_reduce_fusion = (f32[]{:T(128)}, f32[]{:T(128)}, f32[]{:T(128)}, f32[1,512,4096]{1,2,0:T(8,128)}) fusion(bf16[1,512,4096]{1,2,0:T(8,128)(2,1)} %copy.40, f32[]{:T(128)} %bitcast.44, bf16[768,4096]{1,0:T(8,128)(2,1)} %all-gather.3.cloned.1.call-done, bf16[1,768,512]{2,1,0:T(8,128)(2,1)S(1)} %copy-done), kind=kOutput, calls=%fused_computation.18 | convolution fusion | flops 3240099840 | bytes 19660816 | tf_op jit(solution)/shard_map/dot_general | solution.py:81
  222.9 11.4 %all-reduce.5 = (f32[]{:T(128)}, f32[]{:T(128)}, f32[]{:T(128)}) all-reduce(f32[]{:T(128)} %get-tuple-element.17, f32[]{:T(128)} %get-tuple-element.16, f32[]{:T(128)} %get-tuple-element.15), channel_id=1, replica_groups=mesh['expert_0'=4,'expert_1'=2,'fsdp_0'=4,'fsdp_1'=4] {'expert_0'}, use_global_device_ids=true, to_apply=%region_1.2 | all-reduce | flops 3 | bytes 24 | tf_op jit(solution)/shard_map/psum | solution.py:17
  234.3 3.1 all-reduce.7
  237.4 11.1 %all-reduce.3 = (f32[]{:T(128)}, f32[]{:T(128)}, f32[]{:T(128)}) all-reduce(f32[]{:T(128)} %get-tuple-element.43, f32[]{:T(128)} %get-tuple-element.44, f32[]{:T(128)} %get-tuple-element.45), channel_id=1, replica_groups=mesh['expert_0'=4,'expert_1'=2,'fsdp_0'=4,'fsdp_1'=4] {'fsdp_0'}, use_global_device_ids=true, to_apply=%region_3.4 | all-reduce | flops 3 | bytes 24 | tf_op jit(solution)/shard_map/psum | solution.py:17
  248.5 9.4 %all-reduce.1 = (f32[]{:T(128)}, f32[]{:T(128)}, f32[]{:T(128)}) all-reduce(f32[]{:T(128)} %get-tuple-element.29, f32[]{:T(128)} %get-tuple-element.30, f32[]{:T(128)} %get-tuple-element.31), channel_id=1, replica_groups=mesh['expert_0'=4,'expert_1'=2,'fsdp_0'=4,'fsdp_1'=4] {'fsdp_1'}, use_global_device_ids=true, to_apply=%region_4.5 | all-reduce | flops 3 | bytes 24 | tf_op jit(solution)/shard_map/psum | solution.py:17
  261.8 13.1 %convolution_bitcast_fusion = f32[768,4096]{0,1:T(8,128)} fusion(bf16[1,768,512]{2,1,0:T(8,128)(2,1)S(1)} %copy-done, bf16[1,512,4096]{1,2,0:T(8,128)(2,1)} %copy.40, f32[1,512,4096]{1,2,0:T(8,128)} %get-tuple-element.46, f32[]{:T(128)S(6)} %div.13, f32[]{:T(128)S(6)} %div.12), kind=kOutput, calls=%fused_computation.20 | convolution fusion | flops 3233808384 | bytes 25952264 | tf_op jit(solution)/shard_map/dot_general | solution.py:73
  274.9 12.6 %copy.46 = f32[768,4096]{1,0:T(8,128)} copy(f32[768,4096]{0,1:T(8,128)} %convolution_bitcast_fusion) | data formatting | bytes 25165824
  287.5 0.0 reduce-scatter.7.cloned.1.call-update
  287.5 0.0 all-gather.5.cloned.1.call-start
  287.6 89.8 %reduce-scatter.7.cloned.1.call-done = f32[48,4096]{1,0:T(8,128)} async-done(((f32[768,4096]{1,0:T(8,128)}), f32[48,4096]{1,0:T(8,128)}) %reduce-scatter.7.cloned.1.call-update) | async-done | bytes 786448 | tf_op jit(solution)/shard_map/reduce_scatter | solution.py:72
  377.4 1.2 all_to_all.38
  378.6 20.2 %all_to_all.49 = f32[8,6,4096]{2,1,0:T(8,128)S(1)} all-to-all(f32[8,6,4096]{2,1,0:T(8,128)S(1)} %all_to_all.38), channel_id=1, replica_groups=mesh['expert_0'=4,'expert_1'=2,'fsdp_0'=4,'fsdp_1'=4] {'expert_0','exper..., dimensions={0} | all-to-all | bytes 1572864 | tf_op jit(solution)/shard_map/all_to_all | solution.py:78
  398.8 0.1 all_to_all.40
  398.9 0.5 convolution_multiply_fusion
  399.4 0.8 convolution_convert_fusion
  400.2 0.1 all_to_all.41
  400.4 12.8 %all_to_all.50 = bf16[8,6,4096]{2,1,0:T(8,128)(2,1)S(1)} all-to-all(bf16[8,6,4096]{2,1,0:T(8,128)(2,1)S(1)} %all_to_all.41), channel_id=1, replica_groups=mesh['expert_0'=4,'expert_1'=2,'fsdp_0'=4,'fsdp_1'=4] {'expert_0','exper..., dimensions={0} | all-to-all | bytes 786432 | tf_op jit(solution)/shard_map/all_to_all | solution.py:80
  413.1 0.9 all_to_all.43
  414.1 0.0 all-gather.5.cloned.1.call-update
  414.1 6.6 %copy.44 = bf16[1,512,4096]{1,2,0:T(8,128)(2,1)} copy(bf16[1,512,4096]{2,1,0:T(8,128)(2,1)} %param.13) | data formatting | bytes 8388608 | tf_op args[6]
  420.7 8.4 %fusion = (f32[]{:T(128)}, f32[]{:T(128)}, f32[]{:T(128)}) fusion(bf16[1,512,4096]{1,2,0:T(8,128)(2,1)} %copy.44, f32[]{:T(128)S(6)} %div.13, f32[1,512,4096]{1,2,0:T(8,128)} %get-tuple-element.46, f32[]{:T(128)S(6)} %div.12, bf16[1,512,4096]{1,2,0:T(8,128)(2,1)} %copy.40), kind=kLoop, calls=%fused_computation.8 | loop fusion | flops 25165824 | bytes 16777236 | tf_op jit(solution)/shard_map/reduce_sum | solution.py:51
  429.0 43.4 %all-gather.5.cloned.1.call-done = bf16[768,4096]{1,0:T(8,128)(2,1)} async-done(((bf16[48,4096]{1,0:T(8,128)(2,1)}), bf16[768,4096]{1,0:T(8,128)(2,1)}) %all-gather.5.cloned.1.call-update) | async-done | bytes 6291472 | tf_op jit(solution)/shard_map/all_gather | solution.py:83
  472.4 10.1 %fusion.8 = f32[]{:T(128)} fusion(bf16[768,4096]{1,0:T(8,128)(2,1)} %all-gather.5.cloned.1.call-done, f32[]{:T(128)} %bitcast.45, bf16[1,768,512]{2,1,0:T(8,128)(2,1)S(1)} %copy-done, f32[]{:T(128)S(6)} %div.13, f32[1,512,4096]{1,2,0:T(8,128)} %get-tuple-element.46, f32[]{:T(128)S(6)} %div.12, bf16[1,512,4096]{1,2,0:T(8,128)(2,1)} %copy.40), kind=kOutput, calls=%fused_computation.17 | convolution fusion | flops 3240099840 | bytes 19660816 | tf_op jit(solution)/shard_map/dot_general | solution.py:81
  482.5 11.4 %all-reduce.4 = (f32[]{:T(128)}, f32[]{:T(128)}, f32[]{:T(128)}, f32[]{:T(128)}) all-reduce(f32[]{:T(128)} %get-tuple-element.13, f32[]{:T(128)} %fusion.8, f32[]{:T(128)} %get-tuple-element.14, f32[]{:T(128)} %get-tuple-element.12), channel_id=1, replica_groups=mesh['expert_0'=4,'expert_1'=2,'fsdp_0'=4,'fsdp_1'=4] {'expert_0'}, use_global_device_ids=true, to_apply=%region_15.16 | all-reduce | flops 4 | bytes 32 | tf_op jit(solution)/shard_map/psum | solution.py:17
  493.9 3.2 all-reduce.6
  497.0 11.1 %all-reduce.2 = (f32[]{:T(128)}, f32[]{:T(128)}, f32[]{:T(128)}, f32[]{:T(128)}) all-reduce(f32[]{:T(128)} %get-tuple-element.39, f32[]{:T(128)} %get-tuple-element.40, f32[]{:T(128)} %get-tuple-element.41, f32[]{:T(128)} %get-tuple-element.42), channel_id=1, replica_groups=mesh['expert_0'=4,'expert_1'=2,'fsdp_0'=4,'fsdp_1'=4] {'fsdp_0'}, use_global_device_ids=true, to_apply=%region_17.18 | all-reduce | flops 4 | bytes 32 | tf_op jit(solution)/shard_map/psum | solution.py:17
  508.1 9.2 %all-reduce = (f32[]{:T(128)}, f32[]{:T(128)}, f32[]{:T(128)}, f32[]{:T(128)}) all-reduce(f32[]{:T(128)} %get-tuple-element.25, f32[]{:T(128)} %get-tuple-element.26, f32[]{:T(128)} %get-tuple-element.27, f32[]{:T(128)} %get-tuple-element.28), channel_id=1, replica_groups=mesh['expert_0'=4,'expert_1'=2,'fsdp_0'=4,'fsdp_1'=4] {'fsdp_1'}, use_global_device_ids=true, to_apply=%region_18.19 | all-reduce | flops 4 | bytes 32 | tf_op jit(solution)/shard_map/psum | solution.py:17
  518.7 7.7 %fusion.4 = f32[1,512,4096]{1,2,0:T(8,128)} fusion(bf16[1,512,4096]{1,2,0:T(8,128)(2,1)} %copy.40, f32[]{:T(128)S(6)} %div.14, f32[]{:T(128)S(6)} %div.12, f32[]{:T(128)S(6)} %div.13, f32[1,512,4096]{1,2,0:T(8,128)} %get-tuple-element.46), kind=kLoop, calls=%fused_computation.12 | loop fusion | flops 16777216 | bytes 20971532 | tf_op jit(solution)/shard_map/add | solution.py:90
  527.6 8.9 %copy.45 = f32[1,512,4096]{2,1,0:T(8,128)} copy(f32[1,512,4096]{1,2,0:T(8,128)} %fusion.4) | data formatting | bytes 16777216
  (1 shorter events, 0.0 us)
Async XLA Ops:
  7.2 1.1 copy-start
  7.2 107.4 %reduce-scatter.5.cloned.1.call-start = ((), (), s32[]{:S(2)}) async-start(), calls=%async_computation.6 | async-start | bytes 13369344 | tf_op jit(solution)/shard_map/reduce_scatter | solution.py:72
  16.9 104.4 %copy-start.1 = (s32[16,2]{0,1:T(2,128)S(1)}, s32[16,2]{0,1:T(2,128)}, u32[]{:S(2)}) copy-start(s32[16,2]{0,1:T(2,128)} %param.8) | copy-start | bytes 388
  16.9 105.0 %copy-start.3 = (f32[16,2]{0,1:T(2,128)S(1)}, f32[16,2]{0,1:T(2,128)}, u32[]{:S(2)}) copy-start(f32[16,2]{0,1:T(2,128)} %param.9) | copy-start | bytes 388
  16.9 120.4 %copy-start.2 = (f32[16]{0:T(128)S(1)}, f32[16]{0:T(128)}, u32[]{:S(2)}) copy-start(f32[16]{0:T(128)} %param.10) | copy-start | bytes 196
  116.7 20.4 %all-to-all-start = ((f32[8,6,4096]{2,1,0:T(8,128)}), f32[8,6,4096]{2,1,0:T(8,128)S(1)}, u32[]{:S(2)}, u32[]{:S(2)}) async-start(f32[8,6,4096]{2,1,0:T(8,128)} %all_to_all.32), calls=%async_computation.1 | async-start | bytes 2097152 | tf_op jit(solution)/shard_map/all_to_all | solution.py:78
  121.2 89.5 %all-gather.3.cloned.1.call-start = ((), (), s32[]{:S(2)}) async-start(), calls=%async_computation.7 | async-start | bytes 6684672 | tf_op jit(solution)/shard_map/all_gather | solution.py:83
  152.4 225.0 %reduce-scatter.7.cloned.1.call-start = ((), (), s32[]{:S(2)}) async-start(), calls=%async_computation.9 | async-start | bytes 13369344 | tf_op jit(solution)/shard_map/reduce_scatter | solution.py:72
  287.5 184.9 %all-gather.5.cloned.1.call-start = ((), (), s32[]{:S(2)}) async-start(), calls=%async_computation.8 | async-start | bytes 6684672 | tf_op jit(solution)/shard_map/all_gather | solution.py:83
Sparse Core Ops, SparseCore 0:
  17.0 97.4 reduce-scatter.4
  152.5 58.1 all-gather.2
  287.6 89.6 reduce-scatter.6
  414.2 58.1 all-gather.4
where the time goes:
time: 545 us; the launch traced here: 544 us
  waiting for transfers between devices  297 us (54%)
  blocking collectives  116 us (21%)
  matrix products  46.6 us (9%)
  local copies, waits for them, and re-layouts  41.8 us (8%)
  between operations  22 us (4%)
  other arithmetic  16.5 us (3%)
    reduce_scatter x2, waiting for transfers between devices, local(): lax.psum_scatter(jnp.dot(local_hidden, rounded, preferred_element_type=jn...  187 us
    all_gather x2, waiting for transfers between devices, local(): lax.all_gather(returned, FSDP, axis=0, tiled=True)  94.5 us
    psum x8, blocking collectives, by_axis(): array = lax.psum(array, axis)  69.9 us
    unnamed x13, local copies, waits for them, and re-layouts  35.8 us
    all_to_all x2, blocking collectives, local(): lax.all_to_all(leaving, EXPERT, split_axis=0, concat_axis=0, tiled=True)  25.5 us
    dot_general x2, matrix products, local(): lax.dot_general(local_hidden, lax.all_gather(returned, FSDP, axis=0, tile...  22.3 us
    dot_general x2, matrix products, local(): jnp.dot(local_hidden, rounded, preferred_element_type=jnp.float32)  21.6 us
    all_to_all x1, blocking collectives, local(): lax.all_to_all(summed, EXPERT, split_axis=0, concat_axis=0, tiled=True)  20.2 us
  transfers between devices with their start and end apart: 5, of which 5 were waited for; matrix products, arithmetic and copies ran while one was open for 4% of the time, Pallas kernels for 0%

commit v1 on v0

--- a/solution.py
+++ b/solution.py
@@ -80,7 +80,9 @@
         returned = lax.all_to_all(leaving, EXPERT, split_axis=0, concat_axis=0, tiled=True)
         gradient = lax.dot_general(
             local_hidden,
-            lax.all_gather(returned, FSDP, axis=0, tiled=True),
+            jnp.concatenate(
+                lax.all_to_all(jnp.stack([returned] * lax.axis_size(FSDP)), FSDP, 0, 0), axis=0
+            ),
             (((0,), (0,)), ((), ())),
             preferred_element_type=jnp.float32,
         )

time: 545 us -> 626 us (1.15)
  waiting for transfers between devices: 297 us -> 367 us
  starting transfers between devices: 4.58 us -> 13.8 us
    all_to_all x0 -> x2, waiting for transfers between devices: none -> 164 us  [local(): lax.all_to_all(jnp.stack([returned] * lax.axis_size(FSDP)), FSDP, 0, 0)]
    all_gather x2 -> x0, waiting for transfers between devices: 94.5 us -> none  [local(): lax.all_gather(returned, FSDP, axis=0, tiled=True)]
    all_to_all x0 -> x2, starting transfers between devices: none -> 9.26 us  [local(): lax.all_to_all(jnp.stack([returned] * lax.axis_size(FSDP)), FSDP, 0, 0)]
    another operation x0 -> x4, local copies, waits for them, and re-layouts: none -> 7.18 us  [local(): jnp.stack([returned] * lax.axis_size(FSDP))]
where the time goes in v1:
time: 626 us; the launch traced here: 625 us
  waiting for transfers between devices  367 us (59%)
  blocking collectives  112 us (18%)
  local copies, waits for them, and re-layouts  47.1 us (8%)
  matrix products  46.7 us (7%)
  between operations  22.3 us (4%)
  other arithmetic  16.3 us (3%)
  starting transfers between devices  13.8 us (2%)
    reduce_scatter x2, waiting for transfers between devices, local(): lax.psum_scatter(jnp.dot(local_hidden, rounded, preferred_element_type=jn...  188 us
    all_to_all x2, waiting for transfers between devices, local(): lax.all_to_all(jnp.stack([returned] * lax.axis_size(FSDP)), FSDP, 0, 0)  164 us
    psum x8, blocking collectives, by_axis(): array = lax.psum(array, axis)  66.1 us
    unnamed x13, local copies, waits for them, and re-layouts  35.7 us
    all_to_all x2, blocking collectives, local(): lax.all_to_all(leaving, EXPERT, split_axis=0, concat_axis=0, tiled=True)  25.5 us
    dot_general x2, matrix products, local(): lax.dot_general(local_hidden, jnp.concatenate(lax.all_to_all(jnp.stack([r...  22.4 us
    dot_general x2, matrix products, local(): jnp.dot(local_hidden, rounded, preferred_element_type=jnp.float32)  21.6 us
    all_to_all x1, blocking collectives, local(): lax.all_to_all(summed, EXPERT, split_axis=0, concat_axis=0, tiled=True)  20.2 us
  transfers between devices with their start and end apart: 5, of which 5 were waited for; matrix products, arithmetic and copies ran while one was open for 4% of the time, Pallas kernels for 0%

profile of v1, /device:TPU:0, one launch (start us, length us, event | category | flops | bytes accessed | tf_op | source)
XLA Modules:
  0.0 625.0 jit_solution(17462206237105110553)
XLA Ops:
  7.2 0.0 copy-start
  7.2 0.0 reduce-scatter.5.cloned.1.call-start
  7.2 1.1 copy-done
  8.3 8.6 %fusion.10 = f32[768,4096]{1,0:T(8,128)} fusion(bf16[1,512,4096]{2,1,0:T(8,128)(2,1)} %param.12, bf16[1,768,512]{2,1,0:T(8,128)(2,1)S(1)} %copy-done), kind=kOutput, calls=%fused_computation.26 | convolution fusion | flops 3221225472 | bytes 17563648 | tf_op jit(solution)/shard_map/dot_general | solution.py:73
  16.9 0.0 copy-start.1
  16.9 0.0 copy-start.3
  16.9 0.0 copy-start.2
  16.9 0.0 reduce-scatter.5.cloned.1.call-update
  16.9 97.7 %reduce-scatter.5.cloned.1.call-done = f32[48,4096]{1,0:T(8,128)} async-done(((f32[768,4096]{1,0:T(8,128)}), f32[48,4096]{1,0:T(8,128)}) %reduce-scatter.5.cloned.1.call-update) | async-done | bytes 786448 | tf_op jit(solution)/shard_map/reduce_scatter | solution.py:72
  114.5 2.2 all_to_all.34
  116.7 4.4 all-to-all-start
  121.2 0.0 copy-done.1
  121.2 0.1 copy.41
  121.3 0.1 eq.29
  121.3 0.1 fusion.17
  121.4 0.1 reduce_window_sum.11
  121.5 0.2 select_reduce_fusion.1
  121.7 0.1 reduce_sum.89
  121.7 0.1 copy.42
  121.8 0.0 copy-done.3
  121.8 0.1 select_reduce_fusion
  121.9 15.2 %all-to-all-done = f32[8,6,4096]{2,1,0:T(8,128)S(1)} async-done(((f32[8,6,4096]{2,1,0:T(8,128)}), f32[8,6,4096]{2,1,0:T(8,128)S(1)}, u32[]{:S(2)}, u32[]{:S(2)}) %all-to-all-start) | async-done | bytes 786464 | tf_op jit(solution)/shard_map/all_to_all | solution.py:78
  137.1 0.1 all_to_all.36
  137.2 0.0 copy-done.2
  137.2 0.5 convolution_multiply_fusion.1
  137.7 0.8 convolution_convert_fusion.1
  138.6 0.1 all_to_all.37
  138.7 12.8 %all_to_all.52 = bf16[8,6,4096]{2,1,0:T(8,128)(2,1)S(1)} all-to-all(bf16[8,6,4096]{2,1,0:T(8,128)(2,1)S(1)} %all_to_all.37), channel_id=1, replica_groups=mesh['expert_0'=4,'expert_1'=2,'fsdp_0'=4,'fsdp_1'=4] {'expert_0','exper..., dimensions={0} | all-to-all | bytes 786432 | tf_op jit(solution)/shard_map/all_to_all | solution.py:80
  151.5 0.1 stack.8
  151.6 3.5 stack.9
  155.1 4.6 all-to-all-start.2
  159.7 0.0 reduce-scatter.7.cloned.1.call-start
  159.8 6.5 %copy.40 = bf16[1,512,4096]{1,2,0:T(8,128)(2,1)} copy(bf16[1,512,4096]{2,1,0:T(8,128)(2,1)} %param.12) | data formatting | bytes 8388608 | tf_op args[5]
  166.9 85.9 %all-to-all-done.2 = bf16[16,48,4096]{2,1,0:T(8,128)(2,1)} async-done(((bf16[16,48,4096]{2,1,0:T(8,128)(2,1)}), bf16[16,48,4096]{2,1,0:T(8,128)(2,1)}, u32[]{:S(2)}, u32[]{:S(2)}) %all-to-all-start.2) | async-done | bytes 6291488 | tf_op jit(solution)/shard_map/all_to_all | solution.py:84
  252.8 12.3 %multiply_reduce_fusion = (f32[]{:T(128)}, f32[]{:T(128)}, f32[]{:T(128)}, f32[1,512,4096]{1,2,0:T(8,128)}) fusion(bf16[1,512,4096]{1,2,0:T(8,128)(2,1)} %copy.40, f32[]{:T(128)} %bitcast.46, bf16[768,4096]{1,0:T(8,128)(2,1)} %bitcast.2, bf16[1,768,512]{2,1,0:T(8,128)(2,1)S(1)} %copy-done), kind=kOutput, calls=%fused_computation.18 | convolution fusion | flops 3240099840 | bytes 19660816 | tf_op jit(solution)/shard_map/dot_general | solution.py:81
  265.0 9.6 %all-reduce.5 = (f32[]{:T(128)}, f32[]{:T(128)}, f32[]{:T(128)}) all-reduce(f32[]{:T(128)} %get-tuple-element.17, f32[]{:T(128)} %get-tuple-element.16, f32[]{:T(128)} %get-tuple-element.15), channel_id=1, replica_groups=mesh['expert_0'=4,'expert_1'=2,'fsdp_0'=4,'fsdp_1'=4] {'expert_0'}, use_global_device_ids=true, to_apply=%region_1.2 | all-reduce | flops 3 | bytes 24 | tf_op jit(solution)/shard_map/psum | solution.py:17
  274.6 3.1 all-reduce.7
  277.8 10.8 %all-reduce.3 = (f32[]{:T(128)}, f32[]{:T(128)}, f32[]{:T(128)}) all-reduce(f32[]{:T(128)} %get-tuple-element.43, f32[]{:T(128)} %get-tuple-element.44, f32[]{:T(128)} %get-tuple-element.45), channel_id=1, replica_groups=mesh['expert_0'=4,'expert_1'=2,'fsdp_0'=4,'fsdp_1'=4] {'fsdp_0'}, use_global_device_ids=true, to_apply=%region_3.4 | all-reduce | flops 3 | bytes 24 | tf_op jit(solution)/shard_map/psum | solution.py:17
  288.5 9.6 %all-reduce.1 = (f32[]{:T(128)}, f32[]{:T(128)}, f32[]{:T(128)}) all-reduce(f32[]{:T(128)} %get-tuple-element.29, f32[]{:T(128)} %get-tuple-element.30, f32[]{:T(128)} %get-tuple-element.31), channel_id=1, replica_groups=mesh['expert_0'=4,'expert_1'=2,'fsdp_0'=4,'fsdp_1'=4] {'fsdp_1'}, use_global_device_ids=true, to_apply=%region_4.5 | all-reduce | flops 3 | bytes 24 | tf_op jit(solution)/shard_map/psum | solution.py:17
  302.0 13.1 %convolution_bitcast_fusion = f32[768,4096]{0,1:T(8,128)} fusion(bf16[1,768,512]{2,1,0:T(8,128)(2,1)S(1)} %copy-done, bf16[1,512,4096]{1,2,0:T(8,128)(2,1)} %copy.40, f32[1,512,4096]{1,2,0:T(8,128)} %get-tuple-element.46, f32[]{:T(128)S(6)} %div.13, f32[]{:T(128)S(6)} %div.12), kind=kOutput, calls=%fused_computation.20 | convolution fusion | flops 3233808384 | bytes 25952264 | tf_op jit(solution)/shard_map/dot_general | solution.py:73
  315.1 12.6 %copy.46 = f32[768,4096]{1,0:T(8,128)} copy(f32[768,4096]{0,1:T(8,128)} %convolution_bitcast_fusion) | data formatting | bytes 25165824
  327.7 0.0 reduce-scatter.7.cloned.1.call-update
  327.7 89.9 %reduce-scatter.7.cloned.1.call-done = f32[48,4096]{1,0:T(8,128)} async-done(((f32[768,4096]{1,0:T(8,128)}), f32[48,4096]{1,0:T(8,128)}) %reduce-scatter.7.cloned.1.call-update) | async-done | bytes 786448 | tf_op jit(solution)/shard_map/reduce_scatter | solution.py:72
  417.6 1.2 all_to_all.40
  418.8 20.2 %all_to_all.53 = f32[8,6,4096]{2,1,0:T(8,128)S(1)} all-to-all(f32[8,6,4096]{2,1,0:T(8,128)S(1)} %all_to_all.40), channel_id=1, replica_groups=mesh['expert_0'=4,'expert_1'=2,'fsdp_0'=4,'fsdp_1'=4] {'expert_0','exper..., dimensions={0} | all-to-all | bytes 1572864 | tf_op jit(solution)/shard_map/all_to_all | solution.py:78
  439.0 0.1 all_to_all.42
  439.2 0.5 convolution_multiply_fusion
  439.7 0.8 convolution_convert_fusion
  440.5 0.1 all_to_all.43
  440.6 12.8 %all_to_all.54 = bf16[8,6,4096]{2,1,0:T(8,128)(2,1)S(1)} all-to-all(bf16[8,6,4096]{2,1,0:T(8,128)(2,1)S(1)} %all_to_all.43), channel_id=1, replica_groups=mesh['expert_0'=4,'expert_1'=2,'fsdp_0'=4,'fsdp_1'=4] {'expert_0','exper..., dimensions={0} | all-to-all | bytes 786432 | tf_op jit(solution)/shard_map/all_to_all | solution.py:80
  453.4 0.1 stack.10
  453.5 3.4 stack.11
  457.0 4.6 all-to-all-start.5
  461.6 6.5 %copy.44 = bf16[1,512,4096]{1,2,0:T(8,128)(2,1)} copy(bf16[1,512,4096]{2,1,0:T(8,128)(2,1)} %param.13) | data formatting | bytes 8388608 | tf_op args[6]
  468.1 8.2 %fusion = (f32[]{:T(128)}, f32[]{:T(128)}, f32[]{:T(128)}) fusion(bf16[1,512,4096]{1,2,0:T(8,128)(2,1)} %copy.44, f32[]{:T(128)S(6)} %div.13, f32[1,512,4096]{1,2,0:T(8,128)} %get-tuple-element.46, f32[]{:T(128)S(6)} %div.12, bf16[1,512,4096]{1,2,0:T(8,128)(2,1)} %copy.40), kind=kLoop, calls=%fused_computation.8 | loop fusion | flops 25165824 | bytes 16777236 | tf_op jit(solution)/shard_map/reduce_sum | solution.py:51
  476.3 78.4 %all-to-all-done.5 = bf16[16,48,4096]{2,1,0:T(8,128)(2,1)} async-done(((bf16[16,48,4096]{2,1,0:T(8,128)(2,1)}), bf16[16,48,4096]{2,1,0:T(8,128)(2,1)}, u32[]{:S(2)}, u32[]{:S(2)}) %all-to-all-start.5) | async-done | bytes 6291488 | tf_op jit(solution)/shard_map/all_to_all | solution.py:84
  554.7 10.2 %fusion.8 = f32[]{:T(128)} fusion(bf16[768,4096]{1,0:T(8,128)(2,1)} %bitcast.8, f32[]{:T(128)} %bitcast.47, bf16[1,768,512]{2,1,0:T(8,128)(2,1)S(1)} %copy-done, f32[]{:T(128)S(6)} %div.13, f32[1,512,4096]{1,2,0:T(8,128)} %get-tuple-element.46, f32[]{:T(128)S(6)} %div.12, bf16[1,512,4096]{1,2,0:T(8,128)(2,1)} %copy.40), kind=kOutput, calls=%fused_computation.17 | convolution fusion | flops 3240099840 | bytes 19660816 | tf_op jit(solution)/shard_map/dot_general | solution.py:81
  564.8 9.6 %all-reduce.4 = (f32[]{:T(128)}, f32[]{:T(128)}, f32[]{:T(128)}, f32[]{:T(128)}) all-reduce(f32[]{:T(128)} %get-tuple-element.13, f32[]{:T(128)} %fusion.8, f32[]{:T(128)} %get-tuple-element.14, f32[]{:T(128)} %get-tuple-element.12), channel_id=1, replica_groups=mesh['expert_0'=4,'expert_1'=2,'fsdp_0'=4,'fsdp_1'=4] {'expert_0'}, use_global_device_ids=true, to_apply=%region_15.16 | all-reduce | flops 4 | bytes 32 | tf_op jit(solution)/shard_map/psum | solution.py:17
  574.4 3.2 all-reduce.6
  577.6 10.8 %all-reduce.2 = (f32[]{:T(128)}, f32[]{:T(128)}, f32[]{:T(128)}, f32[]{:T(128)}) all-reduce(f32[]{:T(128)} %get-tuple-element.39, f32[]{:T(128)} %get-tuple-element.40, f32[]{:T(128)} %get-tuple-element.41, f32[]{:T(128)} %get-tuple-element.42), channel_id=1, replica_groups=mesh['expert_0'=4,'expert_1'=2,'fsdp_0'=4,'fsdp_1'=4] {'fsdp_0'}, use_global_device_ids=true, to_apply=%region_17.18 | all-reduce | flops 4 | bytes 32 | tf_op jit(solution)/shard_map/psum | solution.py:17
  588.3 9.5 %all-reduce = (f32[]{:T(128)}, f32[]{:T(128)}, f32[]{:T(128)}, f32[]{:T(128)}) all-reduce(f32[]{:T(128)} %get-tuple-element.25, f32[]{:T(128)} %get-tuple-element.26, f32[]{:T(128)} %get-tuple-element.27, f32[]{:T(128)} %get-tuple-element.28), channel_id=1, replica_groups=mesh['expert_0'=4,'expert_1'=2,'fsdp_0'=4,'fsdp_1'=4] {'fsdp_1'}, use_global_device_ids=true, to_apply=%region_18.19 | all-reduce | flops 4 | bytes 32 | tf_op jit(solution)/shard_map/psum | solution.py:17
  599.2 7.7 %fusion.4 = f32[1,512,4096]{1,2,0:T(8,128)} fusion(bf16[1,512,4096]{1,2,0:T(8,128)(2,1)} %copy.40, f32[]{:T(128)S(6)} %div.14, f32[]{:T(128)S(6)} %div.12, f32[]{:T(128)S(6)} %div.13, f32[1,512,4096]{1,2,0:T(8,128)} %get-tuple-element.46), kind=kLoop, calls=%fused_computation.12 | loop fusion | flops 16777216 | bytes 20971532 | tf_op jit(solution)/shard_map/add | solution.py:92
  608.1 8.9 %copy.45 = f32[1,512,4096]{2,1,0:T(8,128)} copy(f32[1,512,4096]{1,2,0:T(8,128)} %fusion.4) | data formatting | bytes 16777216
  (1 shorter events, 0.0 us)
Async XLA Ops:
  7.2 1.1 copy-start
  7.2 107.4 %reduce-scatter.5.cloned.1.call-start = ((), (), s32[]{:S(2)}) async-start(), calls=%async_computation.8 | async-start | bytes 13369344 | tf_op jit(solution)/shard_map/reduce_scatter | solution.py:72
  16.9 104.3 %copy-start.1 = (s32[16,2]{0,1:T(2,128)S(1)}, s32[16,2]{0,1:T(2,128)}, u32[]{:S(2)}) copy-start(s32[16,2]{0,1:T(2,128)} %param.8) | copy-start | bytes 388
  16.9 105.0 %copy-start.3 = (f32[16,2]{0,1:T(2,128)S(1)}, f32[16,2]{0,1:T(2,128)}, u32[]{:S(2)}) copy-start(f32[16,2]{0,1:T(2,128)} %param.9) | copy-start | bytes 388
  16.9 120.4 %copy-start.2 = (f32[16]{0:T(128)S(1)}, f32[16]{0:T(128)}, u32[]{:S(2)}) copy-start(f32[16]{0:T(128)} %param.10) | copy-start | bytes 196
  116.7 20.4 %all-to-all-start = ((f32[8,6,4096]{2,1,0:T(8,128)}), f32[8,6,4096]{2,1,0:T(8,128)S(1)}, u32[]{:S(2)}, u32[]{:S(2)}) async-start(f32[8,6,4096]{2,1,0:T(8,128)} %all_to_all.34), calls=%async_computation.1 | async-start | bytes 2097152 | tf_op jit(solution)/shard_map/all_to_all | solution.py:78
  155.1 97.7 %all-to-all-start.2 = ((bf16[16,48,4096]{2,1,0:T(8,128)(2,1)}), bf16[16,48,4096]{2,1,0:T(8,128)(2,1)}, u32[]{:S(2)}, u32[]{:S(2)}) async-start(bf16[16,48,4096]{2,1,0:T(8,128)(2,1)} %stack.9), calls=%async_computation.3 | async-start | bytes 12582912 | tf_op jit(solution)/shard_map/all_to_all | solution.py:84
  159.7 257.9 %reduce-scatter.7.cloned.1.call-start = ((), (), s32[]{:S(2)}) async-start(), calls=%async_computation.9 | async-start | bytes 13369344 | tf_op jit(solution)/shard_map/reduce_scatter | solution.py:72
  457.0 97.7 %all-to-all-start.5 = ((bf16[16,48,4096]{2,1,0:T(8,128)(2,1)}), bf16[16,48,4096]{2,1,0:T(8,128)(2,1)}, u32[]{:S(2)}, u32[]{:S(2)}) async-start(bf16[16,48,4096]{2,1,0:T(8,128)(2,1)} %stack.11), calls=%async_computation.6 | async-start | bytes 12582912 | tf_op jit(solution)/shard_map/all_to_all | solution.py:84
Sparse Core Ops, SparseCore 0:
  17.0 97.4 reduce-scatter.4
  327.9 89.7 reduce-scatter.6
